TPU v7x, 1024 devices: a whole 4x8x16 slice. The times are simulated.
1024 devices in a mesh: dp: 16 (over y, x_hi), expert: 64 (over z, x_lo, core).
Axes of the slice: x: 4 (x_hi: 2, x_lo: 2; x = x_hi * 2 + x_lo), y: 8, z: 16, core: 2. Of those that a mesh axis runs over, the one named last changes fastest.
Arguments:
- tokens: bfloat16 [2048, 4096], P('expert', 'dp'), may hold values from -6 to 6
- cotangent: bfloat16 [2048, 4096], P('expert', 'dp'), may hold values from -6 to 6
- expert_ids: int32 [2048, 8], P('expert'), may hold values from 0 to 47, all different within a row; in each aligned block of 32 rows (0 to 31, 32 to 63, ...) at most 6 rows name the same one
- gate_weights: float32 [2048, 8], P('expert'), may hold values from 0.2 to 1
- slot_table: int32 [64], replicated, may hold values from 0 to 47, as said below
- split_count: int32 [48], replicated, may hold values from 0 to 64
- w_gate: bfloat16 [64, 4096, 768], P('expert', 'dp'), may hold values from -0.09375 to 0.09375
- w_up: bfloat16 [64, 4096, 768], P('expert', 'dp'), may hold values from -0.09375 to 0.09375
- w_down: bfloat16 [64, 768, 4096], P('expert', None, 'dp'), may hold values from -0.21875 to 0.21875
Outputs:
- mixed: bfloat16 [2048, 4096], P('expert', 'dp')
- token_grad: bfloat16 [2048, 4096], P('expert', 'dp')
- gate_grad: bfloat16 [64, 4096, 768], P('expert', 'dp')
- up_grad: bfloat16 [64, 4096, 768], P('expert', 'dp')
- down_grad: bfloat16 [64, 768, 4096], P('expert', None, 'dp')
Inputs may be any that keep to these rules, and one draw needn't show every extreme that they name: `expert_ids`: in the rows of one device (aligned blocks of 32 rows), no expert is named more than 6 times. `slot_table`: every expert is held by one or two slots; exactly 16 experts are held by two, and those sit on slots s and s + 32 with s below 32.
All inputs are finite; a program needn't handle non-finite values.
Results may differ from a plain program's by a relative error of at most 0.028.
Values may be sent and summed in bfloat16 or wider, within the bound.
A program may use at most 32 MiB of HBM per device.

v0:
```python
import jax
import jax.numpy as jnp
from jax import lax
from jax.sharding import PartitionSpec as P


def in_one_piece(arrays, axis, split_dim, concat_dim, along):
    both = jnp.concatenate(arrays, axis=along)
    out, at, gathered = (
        lax.all_to_all(both, axis, split_axis=split_dim, concat_axis=concat_dim, tiled=True),
        0,
        [],
    )
    for a in arrays:
        gathered.append(lax.slice_in_dim(out, at, at + a.shape[along], axis=along))
        at += a.shape[along]
    return tuple(gathered)


def cut_along(value, dim, devices):
    before, after = (value.shape[:dim], value.shape[dim + 1 :])
    return jnp.moveaxis(value.reshape(*before, devices, -1, *after), dim, 0)


def sent_and_summed(value, axis, dim):
    devices = lax.axis_size(axis)
    pieces = lax.all_to_all(cut_along(value, dim, devices), axis, 0, 0, tiled=True)
    return jnp.sum(pieces.astype(jnp.float32), axis=0)


def side_by_side(arrays, axis, dim, along):
    ends, at = ([], 0)
    for a in arrays[:-1]:
        at += a.shape[along]
        ends.append(at)
    both = jnp.concatenate(arrays, axis=along)
    return tuple(jnp.split(sent_and_summed(both, axis, dim), ends, axis=along))


def from_everyone(value, axis):
    devices = lax.axis_size(axis)
    return lax.all_to_all(
        jnp.broadcast_to(value[None], (devices, *value.shape)), axis, 0, 0, tiled=True
    )


def laid_out(pieces, dim):
    dims = list(pieces.shape[1:])
    dims[dim] *= pieces.shape[0]
    return jnp.moveaxis(pieces, 0, dim).reshape(dims)


def gathered_copies(value, axis, dim):
    pieces = from_everyone(value, axis)
    return laid_out(pieces, dim)


def in_one_piece_2(arrays, axis, dim, along):
    ends, at = ([], 0)
    for a in arrays[:-1]:
        at += a.shape[along]
        ends.append(at)
    both = jnp.concatenate(arrays, axis=along)
    return tuple(jnp.split(lax.all_gather(both, axis, axis=dim, tiled=True), ends, axis=along))


def shifted(value, axis, steps):
    count = lax.axis_size(axis)
    pairs = [(source, (source + steps) % count) for source in range(count)]
    return lax.ppermute(value, axis, pairs)


def slot_choice(expert_ids, slot_table, split_count, source):
    slot_count = slot_table.shape[0]
    expert_count = split_count.shape[0]
    slot_iota = jnp.arange(slot_count, dtype=jnp.int32)
    expert_iota = jnp.arange(expert_count, dtype=jnp.int32)
    holds = slot_table[None, :] == expert_iota[:, None]
    lower = jnp.min(jnp.where(holds, slot_iota[None, :], slot_count), axis=1)
    upper = jnp.max(jnp.where(holds, slot_iota[None, :], -1), axis=1)
    chosen = jnp.where(source < split_count, lower, upper)
    flat_ids = expert_ids.reshape(-1)
    matches = flat_ids[:, None] == expert_iota[None, :]
    target = jnp.sum(jnp.where(matches, chosen[None, :], 0), axis=1)
    onehot = (target[:, None] == slot_iota[None, :]).astype(jnp.int32)
    before = jnp.cumsum(onehot, axis=0) - onehot
    position = jnp.sum(before * onehot, axis=1)
    return (target, position)


def swiglu(gate_pre, up_pre):
    return (jax.nn.silu(gate_pre) * up_pre).astype(jnp.bfloat16)


def swiglu_back(gate_pre, up_pre, upstream):
    sigma = jax.nn.sigmoid(gate_pre)
    gate_back = upstream * up_pre * sigma * (1.0 + gate_pre * (1.0 - sigma))
    up_back = upstream * gate_pre * sigma
    return (gate_back.astype(jnp.bfloat16), up_back.astype(jnp.bfloat16))


def row_contract(left, right_mat):
    return lax.dot_general(
        left, right_mat, (((0,), (0,)), ((), ())), preferred_element_type=jnp.float32
    )


def col_contract(left, right_mat):
    return lax.dot_general(
        left, right_mat, (((1,), (1,)), ((), ())), preferred_element_type=jnp.float32
    )


def on_device(
    tokens, cotangent, expert_ids, gate_weights, slot_table, split_count, w_gate, w_up, w_down
):
    slot_count = slot_table.shape[0]
    expert_count = split_count.shape[0]
    token_count, top_k = expert_ids.shape
    shard_width = tokens.shape[1]
    capacity = max(2, (token_count * top_k + expert_count - 1) // expert_count)
    source = lax.axis_index("expert")
    target, position = slot_choice(expert_ids, slot_table, split_count, source)
    destination = target * capacity + position
    slot_iota = jnp.arange(slot_count * capacity, dtype=jnp.int32)
    selector = (slot_iota[:, None] == destination[None, :]).astype(jnp.bfloat16)
    per_token = jnp.sum(selector.reshape(slot_count * capacity, token_count, top_k), axis=2)
    send_rows = jnp.dot(per_token, tokens, preferred_element_type=jnp.float32).astype(jnp.bfloat16)
    scaled = (gate_weights[:, :, None] * cotangent[:, None, :].astype(jnp.float32)).astype(
        jnp.bfloat16
    )
    send_back = jnp.dot(
        selector,
        scaled.reshape(token_count * top_k, shard_width),
        preferred_element_type=jnp.float32,
    ).astype(jnp.bfloat16)
    got_rows, got_back = in_one_piece(
        (
            send_rows.reshape(slot_count, capacity, shard_width),
            send_back.reshape(slot_count, capacity, shard_width),
        ),
        "expert",
        0,
        0,
        1,
    )
    slot_in = got_rows.reshape(-1, shard_width)
    slot_back = got_back.reshape(-1, shard_width)
    gate_mat = w_gate[0]
    up_mat = w_up[0]
    down_mat = w_down[0]
    gate_part = jnp.dot(slot_in, gate_mat, preferred_element_type=jnp.float32)
    up_part = jnp.dot(slot_in, up_mat, preferred_element_type=jnp.float32)
    gate_pre, up_pre = side_by_side(
        (gate_part.astype(jnp.bfloat16), up_part.astype(jnp.bfloat16)), "dp", 0, 1
    )
    hidden_act = gathered_copies(swiglu(gate_pre, up_pre), "dp", 0)
    slot_out = jnp.dot(hidden_act, down_mat, preferred_element_type=jnp.float32).astype(
        jnp.bfloat16
    )
    upstream = sent_and_summed(col_contract(slot_back, down_mat).astype(jnp.bfloat16), "dp", 0)
    gate_share, up_share = swiglu_back(gate_pre, up_pre, upstream)
    gate_back, up_back = in_one_piece_2((gate_share, up_share), "dp", 0, 1)
    grad_gate = row_contract(slot_in, gate_back).astype(jnp.bfloat16)
    grad_up = row_contract(slot_in, up_back).astype(jnp.bfloat16)
    grad_down = row_contract(hidden_act, slot_back).astype(jnp.bfloat16)
    slot_dx = (col_contract(gate_back, gate_mat) + col_contract(up_back, up_mat)).astype(
        jnp.bfloat16
    )
    out_back, dx_back = in_one_piece(
        (
            slot_out.reshape(slot_count, capacity, shard_width),
            slot_dx.reshape(slot_count, capacity, shard_width),
        ),
        "expert",
        0,
        0,
        1,
    )
    out_assign = row_contract(selector, out_back.reshape(-1, shard_width)).reshape(
        token_count, top_k, shard_width
    )
    dx_assign = row_contract(selector, dx_back.reshape(-1, shard_width)).reshape(
        token_count, top_k, shard_width
    )
    mixed = jnp.sum(gate_weights[:, :, None] * out_assign, axis=1).astype(jnp.bfloat16)
    token_grad = jnp.sum(dx_assign, axis=1).astype(jnp.bfloat16)
    half_axis = lax.axis_size("expert") // 2
    own_expert = lax.dynamic_index_in_dim(slot_table, source, 0, keepdims=False)
    partner_slot = (source + half_axis) % slot_count
    partner_expert = lax.dynamic_index_in_dim(slot_table, partner_slot, 0, keepdims=False)
    paired = (own_expert == partner_expert).astype(jnp.float32)
    far_gate, far_up, far_down = shifted((grad_gate, grad_up, grad_down), "expert", half_axis)
    gate_grad = (grad_gate.astype(jnp.float32) + paired * far_gate.astype(jnp.float32)).astype(
        jnp.bfloat16
    )[None]
    up_grad = (grad_up.astype(jnp.float32) + paired * far_up.astype(jnp.float32)).astype(
        jnp.bfloat16
    )[None]
    down_grad = (grad_down.astype(jnp.float32) + paired * far_down.astype(jnp.float32)).astype(
        jnp.bfloat16
    )[None]
    return (mixed, token_grad, gate_grad, up_grad, down_grad)


def solution(mesh):
    return jax.shard_map(
        on_device,
        mesh=mesh,
        in_specs=(
            P("expert", "dp"),
            P("expert", "dp"),
            P("expert", None),
            P("expert", None),
            P(),
            P(),
            P("expert", "dp", None),
            P("expert", "dp", None),
            P("expert", None, "dp"),
        ),
        out_specs=(
            P("expert", "dp"),
            P("expert", "dp"),
            P("expert", "dp", None),
            P("expert", "dp", None),
            P("expert", None, "dp"),
        ),
        check_vma=False,
    )
```

profile of v0, /device:TPU:2, one launch (start us, length us, event | category | flops | bytes accessed | tf_op | source)
XLA Modules:
  0.0 378.8 jit_solution(5201946495146649784)
XLA Ops:
  7.2 0.0 copy-start
  7.2 0.8 select_reduce_fusion.1
  8.0 0.8 copy.19
  8.8 0.1 mul.86
  8.9 0.8 copy.20
  9.6 0.1 eq.96
  9.7 0.7 convert_element_type.109
  10.5 0.7 compare_select_fusion
  11.1 0.1 select_reduce_fusion
  11.2 0.6 reduce-window.6
  11.8 0.2 slice_reduce_fusion
  12.1 0.1 fusion.30
  12.2 0.1 add.46
  12.3 0.2 fusion.21
  12.5 0.3 convolution_convert_fusion.7
  12.8 0.1 reshape.134
  12.8 0.2 convolution_convert_fusion.6
  13.1 0.1 reshape.133
  13.2 0.2 pad_maximum_fusion.1
  13.4 54.1 %all_to_all.25 = bf16[64,12,256]{2,1,0:T(8,128)(2,1)S(1)} all-to-all(bf16[64,12,256]{2,1,0:T(8,128)(2,1)S(1)} %pad_maximum_fusion.1), channel_id=1, replica_groups=mesh['dp'=16,'expert'=64] {'expert'}, dimensions={0} | all-to-all | bytes 786432 | tf_op jit(solution)/shard_map/all_to_all | solution.py:10
  67.5 0.1 fusion.33
  67.6 0.1 reshape.139
  67.7 1.2 convolution_convert_fusion
  68.9 8.9 %all-to-all-start.3 = ((bf16[16,24,768]{2,1,0:T(8,128)(2,1)}), bf16[16,24,768]{2,1,0:T(8,128)(2,1)S(1)}, u32[]{:S(2)}, u32[]{:S(2)}) async-start(bf16[16,24,768]{2,1,0:T(8,128)(2,1)} %bitcast.9), calls=%async_computation.3 | async-start | bytes 1179648 | tf_op jit(solution)/shard_map/all_to_all | solution.py:27
  77.8 0.1 reshape.135
  77.9 0.3 convolution_convert_fusion.1
  78.2 0.3 convolution_convert_fusion.2
  78.6 1.1 pad_maximum_fusion
  79.7 17.5 %all-to-all-done.3 = bf16[16,24,768]{2,1,0:T(8,128)(2,1)S(1)} async-done(((bf16[16,24,768]{2,1,0:T(8,128)(2,1)}), bf16[16,24,768]{2,1,0:T(8,128)(2,1)S(1)}, u32[]{:S(2)}, u32[]{:S(2)}) %all-to-all-start.3) | async-done | bytes 589856 | tf_op jit(solution)/shard_map/all_to_all | solution.py:27
  97.2 3.7 all-to-all-start.1
  100.9 0.0 all-gather.2.cloned.1.call-start
  100.9 0.1 convert_reduce_fusion.1
  101.0 31.8 %all-to-all-done.1 = bf16[16,24,1536]{2,1,0:T(8,128)(2,1)S(1)} async-done(((bf16[16,24,1536]{2,1,0:T(8,128)(2,1)}), bf16[16,24,1536]{2,1,0:T(8,128)(2,1)S(1)}, u32[]{:S(2)}, u32[]{:S(2)}) %all-to-all-start.1) | async-done | bytes 1179680 | tf_op jit(solution)/shard_map/all_to_all | solution.py:27
  132.8 0.2 convert_reduce_fusion
  132.9 0.1 multiply_convert_fusion.1
  133.0 0.6 pad_maximum_fusion.3
  133.6 0.0 all-gather.2.cloned.1.call-update
  133.7 25.3 %all_to_all.26 = bf16[16,24,768]{2,1,0:T(8,128)(2,1)S(1)} all-to-all(bf16[16,24,768]{2,1,0:T(8,128)(2,1)S(1)} %broadcast_in_dim.66), channel_id=1, replica_groups=mesh['dp'=16,'expert'=64] {'dp'}, dimensions={0} | all-to-all | bytes 1179648 | tf_op jit(solution)/shard_map/all_to_all | solution.py:42
  158.9 0.3 convolution_convert_fusion.8
  159.3 0.1 reshape.138
  159.3 57.1 %all-gather.2.cloned.1.call-done = bf16[384,1536]{1,0:T(8,128)(2,1)} async-done(((bf16[24,1536]{1,0:T(8,128)(2,1)}), bf16[384,1536]{1,0:T(8,128)(2,1)}) %all-gather.2.cloned.1.call-update) | async-done | bytes 1179664 | tf_op jit(solution)/shard_map/all_gather | solution.py:64
  216.5 1.5 fusion.5
  218.0 0.4 fusion
  218.4 0.1 reshape.141
  218.5 1.0 pad_maximum_fusion.2
  219.4 14.9 %all-to-all-start.4 = ((bf16[64,12,256]{2,1,0:T(8,128)(2,1)}), bf16[64,12,256]{2,1,0:T(8,128)(2,1)S(1)}, u32[]{:S(2)}, u32[]{:S(2)}) async-start(bf16[64,12,256]{2,1,0:T(8,128)(2,1)} %pad_maximum_fusion.2), calls=%async_computation.4 | async-start | bytes 1048576 | tf_op jit(solution)/shard_map/all_to_all | solution.py:10
  234.4 0.6 fusion.34
  236.3 0.4 convolution_convert_fusion.3
  236.7 12.2 %collective-permute-start.2 = (bf16[768,256]{1,0:T(8,128)(2,1)S(1)}, bf16[768,256]{1,0:T(8,128)(2,1)S(1)}, u32[]{:S(2)}, u32[]{:S(2)}) collective-permute-start(bf16[768,256]{1,0:T(8,128)(2,1)S(1)} %convolution_convert_fusion.3), channel_id=1, source_target_pairs={{0,32},{1,33},{2,34},{3,35},{4,36},{5,37},{6,38},{7,39},{8,40},{9,... | collective-permute-start | bytes 1179656 | tf_op jit(solution)/shard_map/ppermute | solution.py:70
  248.9 0.4 convolution_convert_fusion.4
  249.3 2.4 collective-permute-start.1
  251.7 0.4 convolution_convert_fusion.5
  252.1 12.2 %collective-permute-start = (bf16[256,768]{1,0:T(8,128)(2,1)S(1)}, bf16[256,768]{1,0:T(8,128)(2,1)S(1)}, u32[]{:S(2)}, u32[]{:S(2)}) collective-permute-start(bf16[256,768]{1,0:T(8,128)(2,1)S(1)} %convolution_convert_fusion.5), channel_id=1, source_target_pairs={{0,32},{1,33},{2,34},{3,35},{4,36},{5,37},{6,38},{7,39},{8,40},{9,... | collective-permute-start | bytes 1179656 | tf_op jit(solution)/shard_map/ppermute | solution.py:70
  264.3 25.5 %collective-permute-done.2 = bf16[768,256]{1,0:T(8,128)(2,1)S(1)} collective-permute-done((bf16[768,256]{1,0:T(8,128)(2,1)S(1)}, bf16[768,256]{1,0:T(8,128)(2,1)S(1)}, u32[]{:S(2)}, u32[]{:S(2)}) %collective-permute-start.2) | collective-permute-done | bytes 393248 | tf_op jit(solution)/shard_map/ppermute | solution.py:70
  289.8 0.9 fusion.9
  290.6 25.1 %collective-permute-done.1 = bf16[256,768]{1,0:T(8,128)(2,1)S(1)} collective-permute-done((bf16[256,768]{1,0:T(8,128)(2,1)S(1)}, bf16[256,768]{1,0:T(8,128)(2,1)S(1)}, u32[]{:S(2)}, u32[]{:S(2)}) %collective-permute-start.1) | collective-permute-done | bytes 393248 | tf_op jit(solution)/shard_map/ppermute | solution.py:70
  315.7 0.9 fusion.8
  316.6 52.5 %collective-permute-done = bf16[256,768]{1,0:T(8,128)(2,1)S(1)} collective-permute-done((bf16[256,768]{1,0:T(8,128)(2,1)S(1)}, bf16[256,768]{1,0:T(8,128)(2,1)S(1)}, u32[]{:S(2)}, u32[]{:S(2)}) %collective-permute-start) | collective-permute-done | bytes 393248 | tf_op jit(solution)/shard_map/ppermute | solution.py:70
  369.1 0.9 fusion.7
  369.9 0.1 fusion.32
  370.0 0.1 reshape.146
  370.1 0.9 convolution_reduce_fusion
  371.0 0.1 reshape.145
  371.1 0.9 fusion.1
  (21 shorter events, 0.1 us)
Async XLA Ops:
  7.2 60.5 %copy-start = (bf16[1,768,256]{2,1,0:T(8,128)(2,1)S(1)}, bf16[1,768,256]{2,1,0:T(8,128)(2,1)}, u32[]{:S(2)}) copy-start(bf16[1,768,256]{2,1,0:T(8,128)(2,1)} %param.17) | copy-start | bytes 1179652
  7.2 5.7 %copy-start.6 = (bf16[32,256]{1,0:T(8,128)(2,1)S(1)}, bf16[32,256]{1,0:T(8,128)(2,1)}, u32[]{:S(2)}) copy-start(bf16[32,256]{1,0:T(8,128)(2,1)} %param.9) | copy-start | bytes 49156
  67.7 1.2 copy-start.4
  67.7 10.2 %copy-start.2 = (bf16[1,256,768]{2,1,0:T(8,128)(2,1)S(1)}, bf16[1,256,768]{2,1,0:T(8,128)(2,1)}, u32[]{:S(2)}) copy-start(bf16[1,256,768]{2,1,0:T(8,128)(2,1)} %param.16) | copy-start | bytes 1179652
  68.9 9.3 %copy-start.1 = (bf16[1,256,768]{2,1,0:T(8,128)(2,1)S(1)}, bf16[1,256,768]{2,1,0:T(8,128)(2,1)}, u32[]{:S(2)}) copy-start(bf16[1,256,768]{2,1,0:T(8,128)(2,1)} %param.15) | copy-start | bytes 1179652
  68.9 28.2 %all-to-all-start.3 = ((bf16[16,24,768]{2,1,0:T(8,128)(2,1)}), bf16[16,24,768]{2,1,0:T(8,128)(2,1)S(1)}, u32[]{:S(2)}, u32[]{:S(2)}) async-start(bf16[16,24,768]{2,1,0:T(8,128)(2,1)} %bitcast.9), calls=%async_computation.3 | async-start | bytes 1179648 | tf_op jit(solution)/shard_map/all_to_all | solution.py:27
  97.2 35.6 %all-to-all-start.1 = ((bf16[16,24,1536]{2,1,0:T(8,128)(2,1)}), bf16[16,24,1536]{2,1,0:T(8,128)(2,1)S(1)}, u32[]{:S(2)}, u32[]{:S(2)}) async-start(bf16[16,24,1536]{2,1,0:T(8,128)(2,1)} %bitcast.6), calls=%async_computation.1 | async-start | bytes 2359296 | tf_op jit(solution)/shard_map/all_to_all | solution.py:27
  100.9 115.6 %all-gather.2.cloned.1.call-start = ((), (), s32[]{:S(2)}) async-start(), calls=%async_computation.5 | async-start | bytes 1253376 | tf_op jit(solution)/shard_map/all_gather | solution.py:64
  216.5 1.5 copy-start.3
  218.4 16.0 %copy-start.7 = (s32[64]{0:T(128)S(1)}, s32[64]{0:T(128)}, u32[]{:S(2)}) copy-start(s32[64]{0:T(128)} %param.13) | copy-start | bytes 772
  218.5 17.8 %copy-start.5 = (bf16[384,256]{1,0:T(8,128)(2,1)S(1)}, bf16[384,256]{1,0:T(8,128)(2,1)}, u32[]{:S(2)}) copy-start(bf16[384,256]{1,0:T(8,128)(2,1)} %copy-done.4) | copy-start | bytes 589828
  219.4 150.5 %all-to-all-start.4 = ((bf16[64,12,256]{2,1,0:T(8,128)(2,1)}), bf16[64,12,256]{2,1,0:T(8,128)(2,1)S(1)}, u32[]{:S(2)}, u32[]{:S(2)}) async-start(bf16[64,12,256]{2,1,0:T(8,128)(2,1)} %pad_maximum_fusion.2), calls=%async_computation.4 | async-start | bytes 1048576 | tf_op jit(solution)/shard_map/all_to_all | solution.py:10
  236.7 53.0 %collective-permute-start.2 = (bf16[768,256]{1,0:T(8,128)(2,1)S(1)}, bf16[768,256]{1,0:T(8,128)(2,1)S(1)}, u32[]{:S(2)}, u32[]{:S(2)}) collective-permute-start(bf16[768,256]{1,0:T(8,128)(2,1)S(1)} %convolution_convert_fusion.3), channel_id=1, source_target_pairs={{0,32},{1,33},{2,34},{3,35},{4,36},{5,37},{6,38},{7,39},{8,40},{9,... | collective-permute-start | bytes 1179656 | tf_op jit(solution)/shard_map/ppermute | solution.py:70
  249.3 66.4 %collective-permute-start.1 = (bf16[256,768]{1,0:T(8,128)(2,1)S(1)}, bf16[256,768]{1,0:T(8,128)(2,1)S(1)}, u32[]{:S(2)}, u32[]{:S(2)}) collective-permute-start(bf16[256,768]{1,0:T(8,128)(2,1)S(1)} %convolution_convert_fusion.4), channel_id=1, source_target_pairs={{0,32},{1,33},{2,34},{3,35},{4,36},{5,37},{6,38},{7,39},{8,40},{9,... | collective-permute-start | bytes 1179656 | tf_op jit(solution)/shard_map/ppermute | solution.py:70
  252.1 117.0 %collective-permute-start = (bf16[256,768]{1,0:T(8,128)(2,1)S(1)}, bf16[256,768]{1,0:T(8,128)(2,1)S(1)}, u32[]{:S(2)}, u32[]{:S(2)}) collective-permute-start(bf16[256,768]{1,0:T(8,128)(2,1)S(1)} %convolution_convert_fusion.5), channel_id=1, source_target_pairs={{0,32},{1,33},{2,34},{3,35},{4,36},{5,37},{6,38},{7,39},{8,40},{9,... | collective-permute-start | bytes 1179656 | tf_op jit(solution)/shard_map/ppermute | solution.py:70
Sparse Core Ops, SparseCore 0:
  133.8 82.6 all-gather.1
where the time goes:
time: 380 us; the launch traced here: 379 us
  waiting for transfers between devices  209 us (55%)
  blocking collectives  79.4 us (21%)
  starting transfers between devices  54.3 us (14%)
  between operations  15.7 us (4%)
  other arithmetic  9.06 us (2%)
  matrix products  7.51 us (2%)
    ppermute x3, waiting for transfers between devices, shifted(): return lax.ppermute(value, axis, pairs)  103 us
    all_gather x1, waiting for transfers between devices, in_one_piece_2(): lax.all_gather(both, axis, axis=dim, tiled=True)  57.1 us
    all_to_all x1, blocking collectives, in_one_piece(): lax.all_to_all(both, axis, split_axis=split_dim, concat_axis=concat_dim,...  54.1 us
    all_to_all x2, waiting for transfers between devices, sent_and_summed(): lax.all_to_all(cut_along(value, dim, devices), axis, 0, 0, tiled=True)  49.2 us
    ppermute x3, starting transfers between devices, shifted(): return lax.ppermute(value, axis, pairs)  26.8 us
    all_to_all x1, blocking collectives, from_everyone(): lax.all_to_all(jnp.broadcast_to(value[None], (devices, *value.shape)), ax...  25.3 us
    all_to_all x1, starting transfers between devices, in_one_piece(): lax.all_to_all(both, axis, split_axis=split_dim, concat_axis=concat_dim,...  14.9 us
    all_to_all x2, starting transfers between devices, sent_and_summed(): lax.all_to_all(cut_along(value, dim, devices), axis, 0, 0, tiled=True)  12.6 us
  transfers between devices with their start and end apart: 7, of which 6 were waited for; matrix products, arithmetic and copies ran while one was open for 2% of the time, Pallas kernels for 0%

commit v1 on v0

v1 whole, which is shorter than its diff:
```python
import functools

import jax
import jax.numpy as jnp
from jax import lax
from jax.experimental import pallas as pl
from jax.experimental.pallas import tpu as pltpu
from jax.sharding import PartitionSpec as P

MESH = pl.DeviceIdType.MESH
BF16 = jnp.bfloat16
F32 = jnp.float32
PAD = 8


def contract(a, b, da, db):
    return lax.dot_general(a, b, (((da,), (db,)), ((), ())), preferred_element_type=F32)


def near_order(count):
    return sorted(range(1, count), key=lambda k: (-min(k, count - k), k))


def layer_kernel(
    dims,
    bounds, ids, gates, lane_expert, lane_chosen, tok, cot, wg, wu, wd,
    mixed, tgrad, ggrad, ugrad, dgrad,
    send_tok, send_cot, send_out, send_dx, got_tok, got_cot, got_out, got_dx,
    slot_in, slot_back, w_high, w_low, own_sel,
    part_gu, part_u, xr_gu, xr_u, ys_gu, ys_u, yr_gu, yr_u, share, far, full,
    flat_send, flat_recv, x_send, x_recv, y_send, y_recv, z_send, z_recv,
    gy_send, gy_recv, gx_send, gx_recv,
):
    n_dp, n_exp, cap, top = dims
    n_y = n_dp // 2
    tokens, width = tok.shape
    rows = n_exp * cap
    lanes = n_exp * PAD
    block, cols = share.shape[1:]
    me = lax.axis_index("expert")
    place = lax.axis_index("dp")
    yy = lax.div(place, 2)
    xx = lax.rem(place, 2)
    other_x = 1 - xx
    x_peer = yy * 2 + other_x
    z_peer = lax.rem(me + n_exp // 2, n_exp)

    def y_at(k):
        return lax.rem(yy + k, n_y)

    barrier = pltpu.get_barrier_semaphore()

    def greet(k, carry):
        pl.semaphore_signal(
            barrier, inc=1, device_id={"expert": lax.rem(me + k, n_exp)}, device_id_type=MESH
        )
        return carry

    lax.fori_loop(1, n_exp, greet, 0)
    pl.semaphore_signal(barrier, inc=1, device_id={"dp": x_peer}, device_id_type=MESH)
    for k in range(1, n_y):
        pl.semaphore_signal(barrier, inc=1, device_id={"dp": y_at(k) * 2 + xx}, device_id_type=MESH)

    shape = (tokens, lanes)
    held = jnp.zeros(shape, jnp.int32)
    weight = jnp.zeros(shape, F32)
    slot_expert = jnp.broadcast_to(lane_expert[...], shape)
    for k in range(top):
        hit = jnp.broadcast_to(ids[:, k : k + 1], shape) == slot_expert
        held = jnp.where(hit, 1, held)
        weight = jnp.where(hit, jnp.broadcast_to(gates[:, k : k + 1], shape), weight)
    t_row = lax.broadcasted_iota(jnp.int32, (tokens, tokens), 0)
    t_col = lax.broadcasted_iota(jnp.int32, (tokens, tokens), 1)
    earlier = jnp.where(t_col < t_row, 1.0, 0.0).astype(BF16)
    position = contract(earlier, held.astype(F32).astype(BF16), 1, 0)
    rank = jnp.bitwise_and(lax.broadcasted_iota(jnp.int32, shape, 1), PAD - 1).astype(F32)
    at_rank = jnp.where(position == rank, held, 0).astype(F32)
    chosen = at_rank * jnp.broadcast_to(lane_chosen[...], shape).astype(F32)
    own_weight = chosen * weight
    high = own_weight.astype(BF16)
    w_high[...] = high
    w_low[...] = (own_weight - high.astype(F32)).astype(BF16)
    own_sel[...] = chosen.astype(BF16)
    select = at_rank.astype(BF16)
    send_tok[...] = contract(select, tok[...], 0, 0).reshape(n_exp, PAD, width).astype(BF16)
    row_weight = jnp.sum(at_rank * weight, axis=0, keepdims=True)
    row_weight = jnp.transpose(jnp.broadcast_to(row_weight, (128, lanes)))[:, :1]
    back = contract(select, cot[...], 0, 0) * row_weight
    send_cot[...] = back.reshape(n_exp, PAD, width).astype(BF16)

    pl.semaphore_wait(barrier, n_exp - 1 + 1 + n_y - 1)

    def scatter(src, dst, at):
        def one(i, carry):
            turn = n_exp - i
            half = lax.div(turn + 1, 2)
            odd = lax.rem(turn, 2)
            peer = lax.rem(me + odd * half + (1 - odd) * (n_exp - half), n_exp)
            pltpu.make_async_remote_copy(
                src_ref=src.at[peer],
                dst_ref=dst.at[me],
                send_sem=flat_send.at[at],
                recv_sem=flat_recv.at[at],
                device_id={"expert": peer},
                device_id_type=MESH,
            ).start()
            return carry

        lax.fori_loop(1, n_exp, one, 0)
        dst[me] = src[me]

    def wait_bytes(ref, sem):
        pltpu.make_async_copy(ref, ref, sem).wait()

    def wait_scatter(dst, at):
        wait_bytes(dst.at[pl.ds(0, n_exp - 1)], flat_recv.at[at])

    scatter(send_tok, got_tok, 0)
    scatter(send_cot, got_cot, 1)

    def matching(shape, row_dim):
        row = lax.broadcasted_iota(jnp.int32, shape, row_dim)
        col = lax.broadcasted_iota(jnp.int32, shape, 1 - row_dim)
        rank = jnp.bitwise_and(col, PAD - 1)
        at = jnp.right_shift(col, 3) * cap + rank
        return jnp.where(at == row, jnp.where(rank < cap, 1.0, 0.0), 0.0).astype(BF16)

    def flat(ref):
        return ref[...].astype(F32).reshape(lanes, width).astype(BF16)

    pack = matching((rows, lanes), 0)
    wait_scatter(got_tok, 0)
    slot_in[...] = contract(pack, flat(got_tok), 1, 0).astype(BF16)

    def put(dst, which, value):
        value = value.astype(BF16)
        for h in range(2):
            dst[h, :, which] = value[:, h * cols : (h + 1) * cols].reshape(n_y, block, cols)

    put(part_gu, 0, contract(slot_in[...], wg[...], 1, 0))
    put(part_gu, 1, contract(slot_in[...], wu[...], 1, 0))

    turns = near_order(n_y)

    def x_stage(part, landing, at):
        for k in turns + [0]:
            b = y_at(k)
            pltpu.make_async_remote_copy(
                src_ref=part.at[other_x, b],
                dst_ref=landing.at[b],
                send_sem=x_send.at[at],
                recv_sem=x_recv.at[at, b],
                device_id={"dp": x_peer},
                device_id_type=MESH,
            ).start()

    def x_sum(part, landing, at, b):
        wait_bytes(landing.at[b], x_recv.at[at, b])
        return part[xx, b].astype(F32) + landing[b].astype(F32)

    def y_stage(part, landing, out, there, at):
        for k in turns:
            b = y_at(k)
            out[b] = x_sum(part, landing, at, b).astype(BF16)
            pltpu.make_async_remote_copy(
                src_ref=out.at[b],
                dst_ref=there.at[yy],
                send_sem=y_send.at[at],
                recv_sem=y_recv.at[at],
                device_id={"dp": b * 2 + xx},
                device_id_type=MESH,
            ).start()
        there[yy] = x_sum(part, landing, at, yy).astype(BF16)

    def y_sum(there, at):
        wait_bytes(there.at[pl.ds(0, n_y - 1)], y_recv.at[at])
        total = there[0].astype(F32)
        for b in range(1, n_y):
            total = total + there[b].astype(F32)
        return total

    x_stage(part_gu, xr_gu, 0)
    y_stage(part_gu, xr_gu, ys_gu, yr_gu, 0)

    wait_scatter(got_cot, 1)
    slot_back[...] = contract(pack, flat(got_cot), 1, 0).astype(BF16)
    put(part_u, 0, contract(slot_back[...], wd[...], 1, 1))
    x_stage(part_u, xr_u, 1)
    y_stage(part_u, xr_u, ys_u, yr_u, 1)

    def z_copy(m):
        return pltpu.make_async_remote_copy(
            src_ref=share.at[m],
            dst_ref=far.at[m],
            send_sem=z_send.at[m],
            recv_sem=z_recv.at[m],
            device_id={"expert": z_peer},
            device_id_type=MESH,
        )

    both = y_sum(yr_gu, 0)
    gate_pre, up_pre = both[0], both[1]
    sigma = 1.0 / (1.0 + jnp.exp(-gate_pre))
    share[0] = (gate_pre * sigma * up_pre).astype(BF16)
    z_copy(0).start()
    upstream = y_sum(yr_u, 1)[0]
    share[1] = (upstream * up_pre * sigma * (1.0 + gate_pre * (1.0 - sigma))).astype(BF16)
    share[2] = (upstream * gate_pre * sigma).astype(BF16)
    z_copy(1).start()
    z_copy(2).start()

    row = lax.broadcasted_iota(jnp.int32, (block, cols), 0) + yy * block
    owned = jnp.where(row >= bounds[0], jnp.where(row < bounds[1], 1, 0), 0)

    def to_y(m):
        z_copy(m).wait_recv()
        mine = jnp.where(owned > 0, share[m].astype(F32), far[m].astype(F32))
        full[m, xx, yy] = mine.astype(BF16)
        for k in turns:
            b = y_at(k)
            pltpu.make_async_remote_copy(
                src_ref=full.at[m, xx, yy],
                dst_ref=full.at[m, xx, yy],
                send_sem=gy_send.at[m],
                recv_sem=gy_recv.at[m, yy],
                device_id={"dp": b * 2 + xx},
                device_id_type=MESH,
            ).start()
        to_x(m, yy)

    def to_x(m, b):
        pltpu.make_async_remote_copy(
            src_ref=full.at[m, xx, b],
            dst_ref=full.at[m, xx, b],
            send_sem=gx_send.at[m],
            recv_sem=gx_recv.at[m],
            device_id={"dp": x_peer},
            device_id_type=MESH,
        ).start()

    def pass_on(m):
        for k in reversed(turns):
            b = y_at(k)
            wait_bytes(full.at[m, xx, b], gy_recv.at[m, b])
            to_x(m, b)

    def whole(m, h):
        return full[m, h].reshape(rows, cols)

    def product(m, mat, dim):
        wait_bytes(full.at[m, other_x], gx_recv.at[m])
        total = None
        for h in range(2):
            cut = mat[h * cols : (h + 1) * cols, :] if dim == 0 else mat[:, h * cols : (h + 1) * cols]
            term = contract(whole(m, h), cut, 1, dim)
            total = term if total is None else total + term
        return total

    spread = matching((lanes, rows), 1)

    def give(value, src, dst, at):
        src[...] = contract(spread, value.astype(BF16), 1, 0).reshape(n_exp, PAD, width).astype(BF16)
        scatter(src, dst, at)

    to_y(0)
    to_y(1)
    to_y(2)
    pass_on(0)
    pass_on(1)
    give(product(0, wd, 0), send_out, got_out, 2)
    pass_on(2)
    dx = product(1, wg, 1)
    give(dx + product(2, wu, 1), send_dx, got_dx, 3)
    for h in range(2):
        cut = slice(h * cols, (h + 1) * cols)
        ggrad[:, cut] = contract(slot_in[...], whole(1, h), 0, 0).astype(BF16)
        ugrad[:, cut] = contract(slot_in[...], whole(2, h), 0, 0).astype(BF16)
        dgrad[cut, :] = contract(whole(0, h), slot_back[...], 0, 0).astype(BF16)

    wait_scatter(got_out, 2)
    out_rows = flat(got_out)
    mixed[...] = (contract(w_high[...], out_rows, 1, 0) + contract(w_low[...], out_rows, 1, 0)).astype(BF16)
    wait_scatter(got_dx, 3)
    tgrad[...] = contract(own_sel[...], flat(got_dx), 1, 0).astype(BF16)

    for at, src in enumerate((send_tok, send_cot, send_out, send_dx)):
        wait_bytes(src.at[pl.ds(0, n_exp - 1)], flat_send.at[at])
    for at, (part, out) in enumerate(((part_gu, ys_gu), (part_u, ys_u))):
        wait_bytes(part.at[0], x_send.at[at])
        wait_bytes(out.at[pl.ds(0, n_y - 1)], y_send.at[at])
    for m in range(3):
        z_copy(m).wait_send()
        wait_bytes(full.at[m, xx, pl.ds(0, n_y - 1)], gy_send.at[m])
        wait_bytes(full.at[m, xx], gx_send.at[m])


def on_device(
    tokens, cotangent, expert_ids, gate_weights, slot_table, split_count, w_gate, w_up, w_down
):
    slot_count = slot_table.shape[0]
    expert_count = split_count.shape[0]
    token_count, top_k = expert_ids.shape
    width = tokens.shape[1]
    hidden_width = w_gate.shape[2]
    cap = max(2, (token_count * top_k + expert_count - 1) // expert_count)
    n_dp = lax.axis_size("dp")
    n_exp = slot_count
    source = lax.axis_index("expert")
    half = slot_count // 2
    n_y = n_dp // 2
    rows = n_exp * cap
    block = rows // n_y
    cols = hidden_width // 2
    lanes = n_exp * PAD

    doubled = slot_table == jnp.roll(slot_table, half)
    experts = jnp.arange(expert_count, dtype=jnp.int32)
    split_at = jnp.sum(jnp.where(slot_table[:, None] == experts[None, :], split_count[None, :], 0), axis=1)
    lower = jnp.arange(slot_count, dtype=jnp.int32) < half
    start = jnp.where(doubled & jnp.logical_not(lower), split_at, 0)
    end = jnp.where(doubled & lower, split_at, n_exp)
    chosen = ((source >= start) & (source < end)).astype(jnp.int32)
    lane_expert = jnp.repeat(slot_table, PAD)[None, :]
    lane_chosen = jnp.repeat(chosen, PAD)[None, :]
    bounds = lax.dynamic_index_in_dim(jnp.stack([start, end], 1) * cap, source, 0, keepdims=False)

    vm = pl.BlockSpec(memory_space=pltpu.VMEM)
    message = pltpu.VMEM((n_exp, PAD, width), BF16)

    def halves(*lead):
        return pltpu.VMEM((*lead, block, cols), BF16)

    dma = pltpu.SemaphoreType.DMA
    mixed, tgrad, ggrad, ugrad, dgrad = pl.pallas_call(
        functools.partial(layer_kernel, (n_dp, n_exp, cap, top_k)),
        out_shape=(
            jax.ShapeDtypeStruct((token_count, width), BF16),
            jax.ShapeDtypeStruct((token_count, width), BF16),
            jax.ShapeDtypeStruct((width, hidden_width), BF16),
            jax.ShapeDtypeStruct((width, hidden_width), BF16),
            jax.ShapeDtypeStruct((hidden_width, width), BF16),
        ),
        in_specs=[pl.BlockSpec(memory_space=pltpu.SMEM)] + [vm] * 9,
        out_specs=(vm,) * 5,
        scratch_shapes=[
            *([message] * 8),
            pltpu.VMEM((rows, width), BF16),
            pltpu.VMEM((rows, width), BF16),
            *([pltpu.VMEM((token_count, lanes), BF16)] * 3),
            halves(2, n_y, 2),
            halves(2, n_y, 1),
            *([halves(n_y, 2), halves(n_y, 1)] * 3),
            halves(3),
            halves(3),
            halves(3, 2, n_y),
            dma((4,)),
            dma((4,)),
            dma((2,)),
            dma((2, n_y)),
            dma((2,)),
            dma((2,)),
            dma((3,)),
            dma((3,)),
            dma((3,)),
            dma((3, n_y)),
            dma((3,)),
            dma((3,)),
        ],
        compiler_params=pltpu.CompilerParams(collective_id=0, has_side_effects=True),
        name="expert_layer",
    )(
        bounds, expert_ids, gate_weights, lane_expert, lane_chosen, tokens, cotangent,
        w_gate[0], w_up[0], w_down[0],
    )
    return mixed, tgrad, ggrad[None], ugrad[None], dgrad[None]


def solution(mesh):
    return jax.shard_map(
        on_device,
        mesh=mesh,
        in_specs=(
            P("expert", "dp"),
            P("expert", "dp"),
            P("expert", None),
            P("expert", None),
            P(),
            P(),
            P("expert", "dp", None),
            P("expert", "dp", None),
            P("expert", None, "dp"),
        ),
        out_specs=(
            P("expert", "dp"),
            P("expert", "dp"),
            P("expert", "dp", None),
            P("expert", "dp", None),
            P("expert", None, "dp"),
        ),
        check_vma=False,
    )
```

time: 380 us -> 132 us (0.35)
  the two profiles are of different devices: /device:TPU:2 before, /device:TPU:1 now
where the time goes in v1:
time: 132 us; the launch traced here: 131 us
  Pallas kernels  120 us (91%)
  local copies, waits for them, and re-layouts  9.93 us (8%)
    pallas_call x1, Pallas kernels, on_device(): pl.pallas_call(functools.partial(layer_kernel, (n_dp, n_exp, cap, top_k))...  120 us
    unnamed x21, local copies, waits for them, and re-layouts  7.67 us

profile of v1, /device:TPU:1, one launch (start us, length us, event | category | flops | bytes accessed | tf_op | source)
XLA Modules:
  0.0 131.2 jit_solution(10651301185833520516)
XLA Ops:
  0.6 0.0 copy-start.3
  0.6 0.0 copy-start.6
  0.7 0.6 copy-done.3
  1.3 0.0 copy-done.6
  1.3 0.1 select_reduce_fusion
  1.4 0.1 fusion.2
  1.5 0.1 and_convert_fusion
  1.6 0.0 copy-start.4
  1.6 0.7 dynamic-slice_reduce_fusion.bounds
  2.3 0.0 copy-done.4
  2.3 0.0 copy-start.5
  2.3 0.7 copy.18.ids
  3.0 0.0 copy-done.5
  3.0 0.7 copy.19.gates
  3.7 0.1 broadcast_in_dim.42
  3.7 0.7 broadcast_in_dim_reshape.7.lane_chosen
  4.4 0.1 broadcast_in_dim.41
  4.5 0.7 broadcast_in_dim_reshape.6.lane_expert
  5.2 120.4 %expert_layer.1 = (bf16[32,256]{1,0:T(8,128)(2,1)}, bf16[32,256]{1,0:T(8,128)(2,1)}, bf16[256,768]{1,0:T(8,128)(2,1)}, bf16[256,768]{1,0:T(8,128)(2,1)}, bf16[768,256]{1,0:T(8,128)(2,1)}) custom-call(s32[2]{0:T(128)} %dynamic-slice_reduce_fusion.bounds, s32[32,8]{1,0:T(8,128)} %copy.18.ids, f32[32,8]{1,0:T(8,128)} %copy.19.gates, ...), custom_call_target="tpu_custom_call" | custom-call | tf_op jit(solution)/shard_map/expert_layer/pallas_call | solution.py:334
  125.6 0.0 copy-start.2
  125.6 1.3 %copy.25 = bf16[32,256]{1,0:T(8,128)(2,1)} copy(bf16[32,256]{1,0:T(8,128)(2,1)} %get-tuple-element.26) | data formatting | bytes 32768
  126.9 0.0 copy-done.2
  126.9 0.6 copy.26
  127.5 0.0 copy-start.1
  127.5 1.8 %copy.27 = bf16[1,256,768]{2,1,0:T(8,128)(2,1)} copy(bf16[1,256,768]{2,1,0:T(8,128)(2,1)} %bitcast.12) | data formatting | bytes 786432
  129.3 0.0 copy-done.1
  129.3 0.0 copy-start
  129.3 0.7 copy.28
  130.1 0.4 copy-done
  130.5 0.7 copy.29
  (2 shorter events, 0.0 us)
Async XLA Ops:
  0.6 0.7 copy-start.3
  0.6 0.7 copy-start.6
  1.6 0.7 copy-start.4
  2.3 0.7 copy-start.5
  125.6 1.3 %copy-start.2 = (bf16[32,256]{1,0:T(8,128)(2,1)S(1)}, bf16[32,256]{1,0:T(8,128)(2,1)}, u32[]{:S(2)}) copy-start(bf16[32,256]{1,0:T(8,128)(2,1)} %get-tuple-element.27) | copy-start | bytes 49156
  127.5 1.8 %copy-start.1 = (bf16[256,768]{1,0:T(8,128)(2,1)S(1)}, bf16[256,768]{1,0:T(8,128)(2,1)}, u32[]{:S(2)}) copy-start(bf16[256,768]{1,0:T(8,128)(2,1)} %get-tuple-element.13) | copy-start | bytes 1179652
  129.3 1.1 copy-start

commit v2 on v1

v2 whole, which is shorter than its diff:
```python
import functools

import jax
import jax.numpy as jnp
from jax import lax
from jax.experimental import pallas as pl
from jax.experimental.pallas import tpu as pltpu
from jax.sharding import PartitionSpec as P

MESH = pl.DeviceIdType.MESH
BF16 = jnp.bfloat16
F32 = jnp.float32
PAD = 4
SHIFT = 2


def contract(a, b, da, db):
    return lax.dot_general(a, b, (((da,), (db,)), ((), ())), preferred_element_type=F32)


def near_order(count):
    return sorted(range(1, count), key=lambda k: (-min(k, count - k), k))


def layer_kernel(
    dims,
    table, splits, ids, gates, tok, cot, wg, wu, wd,
    mixed, tgrad, ggrad, ugrad, dgrad,
    send_tok, send_cot, send_out, send_dx, got_tok, got_cot, got_out, got_dx,
    slot_in, slot_back, w_high, w_low, own_sel, turned, limits,
    *rest,
):
    products, landed, passed, terms = (rest[4 * i : 4 * i + 4] for i in range(4))
    share, far, full = (rest[16 + 2 * i : 18 + 2 * i] for i in range(3))
    (
        flat_send, flat_recv, x_send, x_recv, y_send, y_recv, z_send, z_recv,
        gy_send, gy_recv, gx_send, gx_recv,
    ) = rest[22:]
    n_dp, n_exp, cap, top = dims
    assert cap == PAD + 2
    n_y = n_dp // 2
    tokens, width = tok.shape
    rows = n_exp * cap
    lanes = n_exp * PAD
    block = share[0].shape[1]
    widths = [ref.shape[2] for ref in share]
    cols = sum(widths)
    begins = [0, widths[0]]
    me = lax.axis_index("expert")
    place = lax.axis_index("dp")
    yy = lax.div(place, 2)
    xx = lax.rem(place, 2)
    other_x = 1 - xx
    x_peer = yy * 2 + other_x
    z_peer = lax.rem(me + n_exp // 2, n_exp)

    def y_at(k):
        return lax.rem(yy + k, n_y)

    barrier = pltpu.get_barrier_semaphore()

    def greet(k, carry):
        pl.semaphore_signal(
            barrier, inc=1, device_id={"expert": lax.rem(me + k, n_exp)}, device_id_type=MESH
        )
        return carry

    lax.fori_loop(1, n_exp, greet, 0)
    pl.semaphore_signal(barrier, inc=1, device_id={"dp": x_peer}, device_id_type=MESH)
    for k in range(1, n_y):
        pl.semaphore_signal(barrier, inc=1, device_id={"dp": y_at(k) * 2 + xx}, device_id_type=MESH)

    def lane_of_slot(shift):
        slot = lax.broadcasted_iota(jnp.int32, (n_exp, lanes), 0) + shift
        slot = jnp.where(slot >= n_exp, slot - n_exp, slot)
        lane = jnp.right_shift(lax.broadcasted_iota(jnp.int32, (n_exp, lanes), 1), SHIFT)
        return jnp.where(slot == lane, 1.0, 0.0).astype(BF16)

    def small(ref):
        return jnp.broadcast_to(ref[...].astype(F32), (8, ref.shape[1])).astype(BF16)

    slot_expert = contract(small(table), lane_of_slot(0), 1, 0)
    other_expert = contract(small(table), lane_of_slot(n_exp // 2), 1, 0)
    experts = splits.shape[1]
    expert = lax.broadcasted_iota(jnp.int32, (experts, lanes), 0).astype(F32)
    named = jnp.where(expert == jnp.broadcast_to(slot_expert[:1], (experts, lanes)), 1.0, 0.0)
    split_at = contract(small(splits), named.astype(BF16), 1, 0)
    lane = lax.broadcasted_iota(jnp.int32, (8, lanes), 1)
    alone = slot_expert != other_expert
    start = jnp.where(alone, 0.0, jnp.where(lane < lanes // 2, 0.0, split_at))
    end = jnp.where(alone, float(n_exp), jnp.where(lane < lanes // 2, split_at, float(n_exp)))
    mine = me.astype(F32)
    lane_chosen = jnp.where(start <= mine, jnp.where(mine < end, 1.0, 0.0), 0.0)
    for i, limit in enumerate((start, end)):
        at_me = jnp.sum(jnp.where(lane == me * PAD, limit, 0.0), axis=1, keepdims=True)
        limits[i] = jnp.broadcast_to(at_me * cap, (8, cols))

    turned[...] = jnp.zeros(turned.shape, F32)
    turned[0:top, 0:tokens] = ids[...].astype(F32)
    turned[top : 2 * top, 0:tokens] = gates[...]
    columns = jnp.transpose(turned[...])[:tokens]
    shape = (tokens, lanes)
    held = jnp.zeros(shape, F32)
    weight = jnp.zeros(shape, F32)
    wanted = jnp.broadcast_to(slot_expert[:1], shape)
    for k in range(top):
        hit = jnp.broadcast_to(columns[:, k : k + 1], shape) == wanted
        held = jnp.where(hit, 1.0, held)
        weight = jnp.where(hit, jnp.broadcast_to(columns[:, top + k : top + k + 1], shape), weight)
    t_row = lax.broadcasted_iota(jnp.int32, (tokens, tokens), 0)
    t_col = lax.broadcasted_iota(jnp.int32, (tokens, tokens), 1)
    earlier = jnp.where(t_col < t_row, 1.0, 0.0).astype(BF16)
    position = contract(earlier, held.astype(BF16), 1, 0)
    turn = jnp.bitwise_and(lax.broadcasted_iota(jnp.int32, shape, 1), PAD - 1)
    ranks = (turn, jnp.bitwise_and(turn, 1) + PAD)
    at_rank = [jnp.where(position == rank.astype(F32), held, 0.0) for rank in ranks]
    left = jnp.where(turn < 2, 1.0, 0.0)
    at_rank = [at_rank[0], at_rank[1] * left, at_rank[1] * (1.0 - left)]
    chosen = jnp.broadcast_to(lane_chosen[:1], shape)
    for i, at in enumerate(at_rank):
        own_weight = at * chosen * weight
        high = own_weight.astype(BF16)
        w_high[i] = high
        w_low[i] = (own_weight - high.astype(F32)).astype(BF16)
        own_sel[i] = (at * chosen).astype(BF16)
    piece = width // 2

    def folded(picks, value, da):
        whole_rows = contract(picks[0], value, da, 0)
        halves = contract(picks[1], value[:, :piece], da, 0) + contract(picks[2], value[:, piece:], da, 0)
        return whole_rows, halves

    def message(whole_rows, halves):
        both = jnp.concatenate([whole_rows, halves], axis=1)
        return both.reshape(n_exp, PAD, width + piece).astype(BF16)

    picks = [at.astype(BF16) for at in at_rank]
    send_tok[...] = message(*folded(picks, tok[...], 0))

    def row_weight(at):
        row = jnp.sum(at * weight, axis=0, keepdims=True)
        return jnp.transpose(jnp.broadcast_to(row, (128, lanes)))[:, :1]

    whole_rows, halves = folded(picks, cot[...], 0)
    send_cot[...] = message(
        whole_rows * row_weight(at_rank[0]), halves * row_weight(at_rank[1] + at_rank[2])
    )

    pl.semaphore_wait(barrier, n_exp - 1 + 1 + n_y - 1)

    def scatter(src, dst, at):
        def one(i, carry):
            turn = n_exp - i
            half = lax.div(turn + 1, 2)
            odd = lax.rem(turn, 2)
            peer = lax.rem(me + odd * half + (1 - odd) * (n_exp - half), n_exp)
            pltpu.make_async_remote_copy(
                src_ref=src.at[peer],
                dst_ref=dst.at[me],
                send_sem=flat_send.at[at],
                recv_sem=flat_recv.at[at],
                device_id={"expert": peer},
                device_id_type=MESH,
            ).start()
            return carry

        lax.fori_loop(1, n_exp, one, 0)
        dst[me] = src[me]

    def wait_bytes(ref, sem):
        pltpu.make_async_copy(ref, ref, sem).wait()

    def wait_scatter(dst, at):
        wait_bytes(dst.at[pl.ds(0, n_exp - 1)], flat_recv.at[at])

    scatter(send_tok, got_tok, 0)
    scatter(send_cot, got_cot, 1)

    def matching(shape, row_dim):
        row = lax.broadcasted_iota(jnp.int32, shape, row_dim)
        col = lax.broadcasted_iota(jnp.int32, shape, 1 - row_dim)
        turn = jnp.bitwise_and(col, PAD - 1)
        first = jnp.right_shift(col, SHIFT) * cap
        ahead = jnp.where(first + turn == row, 1.0, 0.0)
        after = jnp.where(first + jnp.bitwise_and(turn, 1) + PAD == row, 1.0, 0.0)
        left = jnp.where(turn < 2, 1.0, 0.0)
        return [m.astype(BF16) for m in (ahead, after * left, after * (1.0 - left))]

    def flat(ref):
        return ref[...].astype(F32).reshape(lanes, width + piece).astype(BF16)

    def unfolded(picks, pieces):
        ends = [contract(picks[i], pieces[:, width:], 1, 0) for i in (1, 2)]
        return contract(picks[0], pieces[:, :width], 1, 0) + jnp.concatenate(ends, axis=1)

    pack = matching((rows, lanes), 0)
    wait_scatter(got_tok, 0)
    slot_in[...] = unfolded(pack, flat(got_tok)).astype(BF16)

    def put(kind, which, value):
        value = value.astype(BF16)
        for p, begin in enumerate(begins):
            for h in range(2):
                columns = value[:, h * cols + begin : h * cols + begin + widths[p]]
                products[2 * p + kind][h, :, which] = columns.reshape(n_y, block, widths[p])

    put(0, 0, contract(slot_in[...], wg[...], 1, 0))
    put(0, 1, contract(slot_in[...], wu[...], 1, 0))

    turns = near_order(n_y)

    def x_stage(at):
        for k in turns + [0]:
            b = y_at(k)
            pltpu.make_async_remote_copy(
                src_ref=products[at].at[other_x, b],
                dst_ref=landed[at].at[b],
                send_sem=x_send.at[at],
                recv_sem=x_recv.at[at, b],
                device_id={"dp": x_peer},
                device_id_type=MESH,
            ).start()

    def x_sum(at, b):
        wait_bytes(landed[at].at[b], x_recv.at[at, b])
        return (products[at][xx, b].astype(F32) + landed[at][b].astype(F32)).astype(BF16)

    def y_stage(at):
        for k in turns:
            b = y_at(k)
            passed[at][b] = x_sum(at, b)
            pltpu.make_async_remote_copy(
                src_ref=passed[at].at[b],
                dst_ref=terms[at].at[yy],
                send_sem=y_send.at[at],
                recv_sem=y_recv.at[at],
                device_id={"dp": b * 2 + xx},
                device_id_type=MESH,
            ).start()
        terms[at][yy] = x_sum(at, yy)

    def y_sum(at):
        wait_bytes(terms[at].at[pl.ds(0, n_y - 1)], y_recv.at[at])
        total = terms[at][0].astype(F32)
        for b in range(1, n_y):
            total = total + terms[at][b].astype(F32)
        return total

    def z_copy(p, m):
        return pltpu.make_async_remote_copy(
            src_ref=share[p].at[m],
            dst_ref=far[p].at[m],
            send_sem=z_send.at[3 * p + m],
            recv_sem=z_recv.at[3 * p + m],
            device_id={"expert": z_peer},
            device_id_type=MESH,
        )

    def forward(p):
        both = y_sum(2 * p)
        gate_pre, up_pre = both[0], both[1]
        sigma = 1.0 / (1.0 + jnp.exp(-gate_pre))
        share[p][0] = (gate_pre * sigma * up_pre).astype(BF16)
        z_copy(p, 0).start()
        return gate_pre, up_pre, sigma

    def backward(p, gate_pre, up_pre, sigma):
        upstream = y_sum(2 * p + 1)[0]
        share[p][1] = (upstream * up_pre * sigma * (1.0 + gate_pre * (1.0 - sigma))).astype(BF16)
        z_copy(p, 1).start()
        share[p][2] = (upstream * gate_pre * sigma).astype(BF16)
        z_copy(p, 2).start()

    x_stage(0)
    y_stage(0)
    wait_scatter(got_cot, 1)
    slot_back[...] = unfolded(pack, flat(got_cot)).astype(BF16)
    put(1, 0, contract(slot_back[...], wd[...], 1, 1))
    x_stage(1)
    x_stage(2)
    x_stage(3)
    y_stage(1)
    kept = forward(0)
    y_stage(2)
    backward(0, *kept)
    y_stage(3)
    kept = forward(1)

    row = (lax.broadcasted_iota(jnp.int32, (block, cols), 0) + yy * block).astype(F32)
    first = jnp.broadcast_to(limits[0, :1], (block, cols))
    last = jnp.broadcast_to(limits[1, :1], (block, cols))
    owned = jnp.where(row >= first, jnp.where(row < last, 1, 0), 0)

    def to_y(p, m):
        z_copy(p, m).wait_recv()
        mine = jnp.where(owned[:, : widths[p]] > 0, share[p][m].astype(F32), far[p][m].astype(F32))
        full[p][m, xx, yy] = mine.astype(BF16)
        for k in turns:
            b = y_at(k)
            pltpu.make_async_remote_copy(
                src_ref=full[p].at[m, xx, yy],
                dst_ref=full[p].at[m, xx, yy],
                send_sem=gy_send.at[3 * p + m],
                recv_sem=gy_recv.at[3 * p + m, yy],
                device_id={"dp": b * 2 + xx},
                device_id_type=MESH,
            ).start()
        to_x(p, m, yy)

    def to_x(p, m, b):
        pltpu.make_async_remote_copy(
            src_ref=full[p].at[m, xx, b],
            dst_ref=full[p].at[m, xx, b],
            send_sem=gx_send.at[3 * p + m],
            recv_sem=gx_recv.at[3 * p + m],
            device_id={"dp": x_peer},
            device_id_type=MESH,
        ).start()

    def pass_on(p, m):
        for k in reversed(turns):
            b = y_at(k)
            wait_bytes(full[p].at[m, xx, b], gy_recv.at[3 * p + m, b])
            to_x(p, m, b)

    def whole(p, m, h):
        return full[p][m, h].reshape(rows, widths[p])

    def span(p, h):
        return slice(h * cols + begins[p], h * cols + begins[p] + widths[p])

    pieces_of = [(p, h) for p in range(2) for h in range(2)]

    def product(m, mat, dim):
        for p in range(2):
            wait_bytes(full[p].at[m, other_x], gx_recv.at[3 * p + m])
        total = None
        for p, h in pieces_of:
            cut = mat[span(p, h), :] if dim == 0 else mat[:, span(p, h)]
            term = contract(whole(p, m, h), cut, 1, dim)
            total = term if total is None else total + term
        return total

    spread = matching((lanes, rows), 1)

    def give(value, src, dst, at):
        src[...] = message(*folded(spread, value.astype(BF16), 1))
        scatter(src, dst, at)

    to_y(0, 0)
    backward(1, *kept)
    to_y(0, 1)
    to_y(0, 2)
    pass_on(0, 0)
    pass_on(0, 1)
    to_y(1, 0)
    pass_on(0, 2)
    to_y(1, 1)
    to_y(1, 2)
    pass_on(1, 0)
    give(product(0, wd, 0), send_out, got_out, 2)
    pass_on(1, 1)
    pass_on(1, 2)
    dx = product(1, wg, 1)
    give(dx + product(2, wu, 1), send_dx, got_dx, 3)
    for p, h in pieces_of:
        ggrad[:, span(p, h)] = contract(slot_in[...], whole(p, 1, h), 0, 0).astype(BF16)
        ugrad[:, span(p, h)] = contract(slot_in[...], whole(p, 2, h), 0, 0).astype(BF16)
        dgrad[span(p, h), :] = contract(whole(p, 0, h), slot_back[...], 0, 0).astype(BF16)

    wait_scatter(got_out, 2)
    out_rows = flat(got_out)
    mixed[...] = (unfolded(w_high, out_rows) + unfolded(w_low, out_rows)).astype(BF16)
    wait_scatter(got_dx, 3)
    tgrad[...] = unfolded(own_sel, flat(got_dx)).astype(BF16)

    for at, src in enumerate((send_tok, send_cot, send_out, send_dx)):
        wait_bytes(src.at[pl.ds(0, n_exp - 1)], flat_send.at[at])
    for at in range(4):
        wait_bytes(products[at].at[0], x_send.at[at])
        wait_bytes(passed[at].at[pl.ds(0, n_y - 1)], y_send.at[at])
    for p in range(2):
        for m in range(3):
            z_copy(p, m).wait_send()
            wait_bytes(full[p].at[m, xx, pl.ds(0, n_y - 1)], gy_send.at[3 * p + m])
            wait_bytes(full[p].at[m, xx], gx_send.at[3 * p + m])


def hand_over(*refs):
    count = (len(refs) - 2) // 3
    src, dst, held = refs[:count], refs[count : 2 * count], refs[2 * count : 3 * count]
    taken, given = refs[3 * count :]
    first = [pltpu.make_async_copy(src[i], held[i], taken.at[i]) for i in range(count)]
    then = [pltpu.make_async_copy(held[i], dst[i], given.at[i]) for i in range(count)]
    for copy in first:
        copy.start()
    for i in range(count):
        first[i].wait()
        then[i].start()
    for copy in then:
        copy.wait()


def on_device(
    tokens, cotangent, expert_ids, gate_weights, slot_table, split_count, w_gate, w_up, w_down
):
    slot_count = slot_table.shape[0]
    expert_count = split_count.shape[0]
    token_count, top_k = expert_ids.shape
    width = tokens.shape[1]
    hidden_width = w_gate.shape[2]
    cap = max(2, (token_count * top_k + expert_count - 1) // expert_count)
    n_dp = lax.axis_size("dp")
    n_exp = slot_count
    n_y = n_dp // 2
    rows = n_exp * cap
    block = rows // n_y
    cols = hidden_width // 2
    lanes = n_exp * PAD

    vm = pl.BlockSpec(memory_space=pltpu.VMEM)
    message = pltpu.VMEM((n_exp, PAD, width + width // 2), BF16)

    widths = (cols - cols // 3, cols // 3)

    def halves(*lead):
        return [pltpu.VMEM((*lead, block, width), BF16) for width in widths]

    def kinds(*lead):
        pairs = zip(halves(*lead, 2), halves(*lead, 1), strict=True)
        return [buffer for pair in pairs for buffer in pair]

    dma = pltpu.SemaphoreType.DMA
    results = pl.pallas_call(
        functools.partial(layer_kernel, (n_dp, n_exp, cap, top_k)),
        out_shape=(
            jax.ShapeDtypeStruct((token_count, width), BF16),
            jax.ShapeDtypeStruct((token_count, width), BF16),
            jax.ShapeDtypeStruct((width, hidden_width), BF16),
            jax.ShapeDtypeStruct((width, hidden_width), BF16),
            jax.ShapeDtypeStruct((hidden_width, width), BF16),
        ),
        in_specs=[vm] * 9,
        out_specs=(vm,) * 5,
        scratch_shapes=[
            *([message] * 8),
            pltpu.VMEM((rows, width), BF16),
            pltpu.VMEM((rows, width), BF16),
            *([pltpu.VMEM((3, token_count, lanes), BF16)] * 3),
            pltpu.VMEM((128, 128), F32),
            pltpu.VMEM((2, 8, cols), F32),
            *kinds(2, n_y),
            *(kinds(n_y) * 3),
            *halves(3),
            *halves(3),
            *halves(3, 2, n_y),
            dma((4,)),
            dma((4,)),
            dma((4,)),
            dma((4, n_y)),
            dma((4,)),
            dma((4,)),
            dma((6,)),
            dma((6,)),
            dma((6,)),
            dma((6, n_y)),
            dma((6,)),
            dma((6,)),
        ],
        compiler_params=pltpu.CompilerParams(collective_id=0, has_side_effects=True),
        name="expert_layer",
    )(
        slot_table[None], split_count[None], expert_ids.T, gate_weights.T, tokens, cotangent,
        w_gate[0], w_up[0], w_down[0],
    )
    anywhere = pl.BlockSpec(memory_space=pl.ANY)
    mixed, tgrad, ggrad, ugrad, dgrad = pl.pallas_call(
        hand_over,
        out_shape=tuple(jax.ShapeDtypeStruct(r.shape, r.dtype) for r in results),
        in_specs=[anywhere] * 5,
        out_specs=(anywhere,) * 5,
        scratch_shapes=[*(pltpu.VMEM(r.shape, r.dtype) for r in results), dma((5,)), dma((5,))],
        name="hand_over",
    )(*results)
    return mixed, tgrad, ggrad[None], ugrad[None], dgrad[None]


def solution(mesh):
    return jax.shard_map(
        on_device,
        mesh=mesh,
        in_specs=(
            P("expert", "dp"),
            P("expert", "dp"),
            P("expert", None),
            P("expert", None),
            P(),
            P(),
            P("expert", "dp", None),
            P("expert", "dp", None),
            P("expert", None, "dp"),
        ),
        out_specs=(
            P("expert", "dp"),
            P("expert", "dp"),
            P("expert", "dp", None),
            P("expert", "dp", None),
            P("expert", None, "dp"),
        ),
        check_vma=False,
    )
```

time: 132 us -> 114 us (0.86)
  local copies, waits for them, and re-layouts: 9.93 us -> 0 us
  Pallas kernels: 120 us -> 113 us
    pallas_call x1, Pallas kernels: 120 us -> 111 us  [on_device(): pl.pallas_call(functools.partial(layer_kernel, (n_dp, n_exp, cap, top_k))...]
    unnamed x21 -> x0, local copies, waits for them, and re-layouts: 7.67 us -> none
    pallas_call x0 -> x1, Pallas kernels: none -> 2.12 us  [on_device(): pl.pallas_call(hand_over, out_shape=tuple((jax.ShapeDtypeStruct(r.shape,...]
    another operation x2 -> x0, local copies, waits for them, and re-layouts: 1.35 us -> none  [the longest x1 0.68 us: on_device(): lane_chosen = jnp.repeat(chosen, PAD)[None, :]]
where the time goes in v2:
time: 114 us
  Pallas kernels  113 us (99%)
    pallas_call x1, Pallas kernels, on_device(): pl.pallas_call(functools.partial(layer_kernel, (n_dp, n_exp, cap, top_k))...  111 us

profile of v2, /device:TPU:1, one launch (start us, length us, event | category | flops | bytes accessed | tf_op | source)
XLA Modules:
  0.0 113.8 jit_solution(5285884959150760203)
XLA Ops:
  0.6 111.0 %expert_layer.1 = (bf16[32,256]{1,0:T(8,128)(2,1)}, bf16[32,256]{1,0:T(8,128)(2,1)}, bf16[256,768]{1,0:T(8,128)(2,1)}, bf16[256,768]{1,0:T(8,128)(2,1)}, bf16[768,256]{1,0:T(8,128)(2,1)}) custom-call(s32[1,64]{1,0:T(1,128)} %bitcast.15, s32[1,48]{1,0:T(1,128)} %bitcast.16, s32[8,32]{1,0:T(8,128)} %bitcast.13, f32[8,32]{1,0:T(8,128)} %bitcast.14, ...), custom_call_target="tpu_custom_call" | custom-call | tf_op jit(solution)/shard_map/expert_layer/pallas_call | solution.py:434
  111.6 2.1 %hand_over.1 = (bf16[32,256]{1,0:T(8,128)(2,1)}, bf16[32,256]{1,0:T(8,128)(2,1)}, bf16[256,768]{1,0:T(8,128)(2,1)}, bf16[256,768]{1,0:T(8,128)(2,1)}, bf16[768,256]{1,0:T(8,128)(2,1)}) custom-call(bf16[32,256]{1,0:T(8,128)(2,1)} %get-tuple-element.15.refs_0_, bf16[32,256]{1,0:T(8,128)(2,1)} %get-tuple-element.16.refs_1_, ...), custom_call_target="tpu_custom_call" | custom-call | tf_op jit(solution)/shard_map/hand_over/pallas_call | solution.py:477

commit v3 on v2

--- a/solution.py
+++ b/solution.py
@@ -272,19 +272,19 @@
         z_copy(p, 2).start()
 
     x_stage(0)
+    x_stage(2)
     y_stage(0)
     wait_scatter(got_cot, 1)
     slot_back[...] = unfolded(pack, flat(got_cot)).astype(BF16)
     put(1, 0, contract(slot_back[...], wd[...], 1, 1))
     x_stage(1)
-    x_stage(2)
     x_stage(3)
+    y_stage(2)
+    kept = [forward(0)]
     y_stage(1)
-    kept = forward(0)
-    y_stage(2)
-    backward(0, *kept)
+    kept.append(forward(1))
     y_stage(3)
-    kept = forward(1)
+    backward(0, *kept[0])
 
     row = (lax.broadcasted_iota(jnp.int32, (block, cols), 0) + yy * block).astype(F32)
     first = jnp.broadcast_to(limits[0, :1], (block, cols))
@@ -348,17 +348,17 @@
         scatter(src, dst, at)
 
     to_y(0, 0)
-    backward(1, *kept)
+    backward(1, *kept[1])
+    to_y(1, 0)
+    pass_on(0, 0)
     to_y(0, 1)
     to_y(0, 2)
-    pass_on(0, 0)
+    pass_on(1, 0)
     pass_on(0, 1)
-    to_y(1, 0)
+    to_y(1, 1)
+    give(product(0, wd, 0), send_out, got_out, 2)
     pass_on(0, 2)
-    to_y(1, 1)
     to_y(1, 2)
-    pass_on(1, 0)
-    give(product(0, wd, 0), send_out, got_out, 2)
     pass_on(1, 1)
     pass_on(1, 2)
     dx = product(1, wg, 1)

time: 114 us -> 108 us (0.947)
  Pallas kernels: 113 us -> 107 us
    pallas_call x1, Pallas kernels: 111 us -> 105 us  [on_device(): pl.pallas_call(functools.partial(layer_kernel, (n_dp, n_exp, cap, top_k))...]
where the time goes in v3:
time: 108 us; the launch traced here: 107 us
  Pallas kernels  107 us (99%)
    pallas_call x1, Pallas kernels, on_device(): pl.pallas_call(functools.partial(layer_kernel, (n_dp, n_exp, cap, top_k))...  105 us

profile of v3, /device:TPU:1, one launch (start us, length us, event | category | flops | bytes accessed | tf_op | source)
XLA Modules:
  0.0 107.5 jit_solution(8812648933611350407)
XLA Ops:
  0.6 104.7 %expert_layer.1 = (bf16[32,256]{1,0:T(8,128)(2,1)}, bf16[32,256]{1,0:T(8,128)(2,1)}, bf16[256,768]{1,0:T(8,128)(2,1)}, bf16[256,768]{1,0:T(8,128)(2,1)}, bf16[768,256]{1,0:T(8,128)(2,1)}) custom-call(s32[1,64]{1,0:T(1,128)} %bitcast.15, s32[1,48]{1,0:T(1,128)} %bitcast.16, s32[8,32]{1,0:T(8,128)} %bitcast.13, f32[8,32]{1,0:T(8,128)} %bitcast.14, ...), custom_call_target="tpu_custom_call" | custom-call | tf_op jit(solution)/shard_map/expert_layer/pallas_call | solution.py:434
  105.3 2.1 %hand_over.1 = (bf16[32,256]{1,0:T(8,128)(2,1)}, bf16[32,256]{1,0:T(8,128)(2,1)}, bf16[256,768]{1,0:T(8,128)(2,1)}, bf16[256,768]{1,0:T(8,128)(2,1)}, bf16[768,256]{1,0:T(8,128)(2,1)}) custom-call(bf16[32,256]{1,0:T(8,128)(2,1)} %get-tuple-element.15.refs_0_, bf16[32,256]{1,0:T(8,128)(2,1)} %get-tuple-element.16.refs_1_, ...), custom_call_target="tpu_custom_call" | custom-call | tf_op jit(solution)/shard_map/hand_over/pallas_call | solution.py:477
